TPU v7x, 256 devices: a whole 4x4x8 slice. The times are simulated.
256 devices in a mesh: tm: 64 (over z, y, x_hi), pair: 4 (over x_lo, core).
Axes of the slice: x: 4 (x_hi: 2, x_lo: 2; x = x_hi * 2 + x_lo), y: 4, z: 8, core: 2. Of those that a mesh axis runs over, the one named last changes fastest.
Arguments:
- x_path: bfloat16 [8, 32768, 512], P('pair', 'tm'), parts along dimension 0, may hold values from -0.19921875 to 0.19921875
- x_anchor: bfloat16 [8, 512], P('pair'), parts along dimension 0, may hold values from -0.19921875 to 0.19921875
- y_steps: bfloat16 [8, 8192, 512], P('pair', 'tm'), parts along dimension 0, may hold values from -0.14941406 to 0.14941406
- left_in: float32 [16, 32768], P('pair', 'tm'), parts along dimension 0, may hold values from 0.5 to 1.5
- bottom_in: float32 [16, 8192], P('pair', 'tm'), parts along dimension 0, may hold values from 0.5 to 1.5
- corner_in: float32 [16, 64], P('pair', 'tm'), parts along dimension 0, may hold values from 0.5 to 1.5
Outputs:
- right_out: float32 [16, 32768], P('pair', 'tm'), parts along dimension 0
- top_out: float32 [16, 49152], P('pair', 'tm'), parts along dimension 0
There are 4 independent parts, one for each index of `pair`. A program takes and returns all parts, laid end to end along the dimension named above; each array names one. Nothing has to cross between parts.
All inputs are finite; a program needn't handle non-finite values.
Results may differ from a plain program's by a relative error of at most 0.00094.
Values may be sent and summed in bfloat16 or wider, within the bound.
A program may use at most 64 MiB of HBM per device.

v0:
```python
import functools

import jax
import jax.numpy as jnp
from jax import lax
from jax.experimental import pallas as pl
from jax.experimental.pallas import tpu as pltpu
from jax.sharding import PartitionSpec as P

MESH = pl.DeviceIdType.MESH
TICKS = 6
HOPS = TICKS - 1
TILE = 128
LEVELS = 4
PAIRS = 4
GROUPS = TILE // 8
F32 = jnp.float32
BF16 = jnp.bfloat16


def iota(shape, axis):
    return lax.broadcasted_iota(jnp.int32, shape, axis)


def tile_row(shape):
    place = iota(shape, 0)
    return (place % 8) * GROUPS + place // 8


def split_dot(rows, weights):
    high = rows.astype(BF16)
    low = (rows - high.astype(F32)).astype(BF16)
    return jnp.dot(jnp.concatenate([high, low], axis=1), weights, preferred_element_type=F32)


def vectors(tile):
    return [tile[8 * j : 8 * j + 8] for j in range(GROUPS)]


def stacked(parts):
    return jnp.concatenate(parts, axis=0)


def before_rows(tile):
    sub = iota((8, TILE), 0)
    running = jnp.zeros((8, TILE), F32)
    sums = []
    for part in vectors(tile):
        sums.append(running)
        running = running + part
    scan = running
    for step in (1, 2, 4):
        scan = scan + jnp.where(sub >= step, pltpu.roll(scan, step, axis=0), 0.0)
    offset = scan - running
    return stacked([s + offset for s in sums])


def all_rows(tile):
    parts = vectors(tile)
    while len(parts) > 1:
        parts = [a + b for a, b in zip(parts[::2], parts[1::2])]
    total = parts[0]
    for step in (4, 2, 1):
        total = total + pltpu.roll(total, step, axis=0)
    return total


def repeated(row):
    return stacked([row] * GROUPS)


def rows_of_pairs(values):
    sub = iota((8, TILE), 0)
    out = values[-1]
    for k in range(len(values) - 2, -1, -1):
        out = jnp.where(sub == k, values[k], out)
    return out


def kernel(
    x_ref, anchor_ref, y_ref, left_ref, bottom_ref, corner_ref, right_ref, top_ref,
    steps, prod, minus, plus, lead, lam, last, edge, corner, tri, ones,
    xs, xgot, ybuf, note, heard,
    xs_send, xs_recv, y_send, y_recv, note_send, note_recv,
):
    count = lax.axis_size("tm")
    me, part = lax.axis_index("tm"), lax.axis_index("pair")
    at_start = me == 0
    next1, next2 = lax.rem(me + 1, count), lax.rem(me + 2, count)
    prev1, prev2 = lax.rem(me + count - 1, count), lax.rem(me + count - 2, count)

    barrier = pltpu.get_barrier_semaphore()
    for other in (prev1, prev2):
        pl.semaphore_signal(barrier, inc=1, device_id=(other, part), device_id_type=MESH)

    for m in range(2):
        tail = x_ref[m, 496:512, :].astype(F32)[15:16]
        for c in range(4):
            xs[m * 4 + c : m * 4 + c + 1, :] = tail[:, c * 128 : (c + 1) * 128]

    def x_copy():
        return pltpu.make_async_remote_copy(
            src_ref=xs, dst_ref=xgot, send_sem=xs_send, recv_sem=xs_recv,
            device_id=(next1, part), device_id_type=MESH,
        )

    def y_copy(source, slot, sem, to):
        return pltpu.make_async_remote_copy(
            src_ref=source, dst_ref=ybuf.at[slot], send_sem=y_send.at[sem], recv_sem=y_recv.at[slot],
            device_id=(to, part), device_id_type=MESH,
        )

    def note_copy(t):
        return pltpu.make_async_remote_copy(
            src_ref=note.at[t], dst_ref=heard.at[t], send_sem=note_send.at[t], recv_sem=note_recv.at[t],
            device_id=(next1, part), device_id_type=MESH,
        )

    pl.semaphore_wait(barrier, 2)
    x_copy().start()
    y_copy(y_ref, 0, 0, next1).start()
    y_copy(y_ref, 1, 1, next2).start()

    from_row = iota((2 * TILE, TILE), 0) % TILE
    tri[...] = jnp.where(from_row < iota((2 * TILE, TILE), 1), 1.0, 0.0).astype(BF16)
    ones[...] = jnp.ones((2 * TILE, TILE), BF16)
    row_here, lane = tile_row((TILE, TILE)), iota((TILE, TILE), 1)
    differ = jnp.where(lane == row_here, 1.0, jnp.where(lane == row_here - 1, -1.0, 0.0)).astype(BF16)
    lane_row = iota((8, TILE), 1)

    for p in range(PAIRS):
        start = jnp.broadcast_to(corner_ref[p : p + 1, 0:1], (8, TILE))
        start = jnp.where(at_start, 1.0, start)
        corner[0, p] = start
        for r in range(LEVELS):
            at = (r + 1) * TILE - 1
            corner[r + 1, p] = jnp.broadcast_to(left_ref[p : p + 1, at : at + 1], (8, TILE))
        bottom = jnp.broadcast_to(bottom_ref[p : p + 1, :], (8, TILE))
        shifted = jnp.where(lane_row == 0, start, pltpu.roll(bottom, 1, axis=1))
        edge[0, p] = jnp.where(at_start, 0.0, bottom - shifted)
    for r in range(LEVELS):
        picked = []
        for p in range(PAIRS):
            row = jnp.broadcast_to(left_ref[p : p + 1, r * TILE : (r + 1) * TILE], (8, TILE)) - corner[r, p]
            picked.append(jnp.where(lane == row_here - 1, repeated(row), 0.0))
        spread = split_dot(stacked(picked), ones[...])
        for p in range(PAIRS):
            lam[r, p] = spread[p * TILE : (p + 1) * TILE]

    def increments(m, r, previous):
        found = jnp.dot(differ, x_ref[m, r * TILE : (r + 1) * TILE, :], preferred_element_type=F32)
        found = jnp.where(iota((TILE, 512), 0) == 0, found - previous, found)
        steps[m, r * TILE : (r + 1) * TILE, :] = found.astype(BF16)

    for m in range(2):
        for r in range(1, LEVELS):
            increments(m, r, x_ref[m, r * TILE - 16 : r * TILE, :].astype(F32)[15:16])
    x_copy().wait_recv()
    for m in range(2):
        came = jnp.concatenate([xgot[m * 4 + c : m * 4 + c + 1, :] for c in range(4)], axis=1)
        increments(m, 0, jnp.where(at_start, anchor_ref[m : m + 1, :].astype(F32), came))

    def prepare(y_of):
        for m in range(2):
            for n in range(2):
                found = lax.dot_general(
                    steps[m], y_of(n), (((1,), (1,)), ((), ())), preferred_element_type=F32
                )
                for r in range(LEVELS):
                    prod[r, 2 * m + n] = found[r * TILE : (r + 1) * TILE]

        def level(r, carry):
            across = split_dot(stacked([prod[r, p] for p in range(PAIRS)]), tri[...])
            for p in range(PAIRS):
                wide = across[p * TILE : (p + 1) * TILE]
                both = before_rows(wide)
                down = before_rows(prod[r, p])
                minus[r, p] = -(both + down)
                plus[r, p] = 1.0 + both
                edge_part = lam[r, p]
                lead[r, p] = edge_part + before_rows(edge_part * wide)
            return carry

        lax.fori_loop(0, LEVELS, level, 0)

    def chain():
        def level(r, carry):
            bottoms = [edge[r, p] for p in range(PAIRS)]
            rows = [repeated(bottoms[p]) * minus[r, p] for p in range(PAIRS)]
            grids, bases = [None] * PAIRS, [None] * PAIRS
            for a, b in ((0, 1), (2, 3)):
                out = split_dot(stacked([rows[a], rows[b], bottoms[a], bottoms[b]]), tri[...])
                for k, p in enumerate((a, b)):
                    low = corner[r, p] + out[2 * TILE + 8 * k : 2 * TILE + 8 * k + 8]
                    low = repeated(low)
                    bases[p] = lam[r, p] + low
                    grids[p] = lead[r, p] + low * plus[r, p] + out[k * TILE : (k + 1) * TILE]
            for sweep in range(2):
                for a, b in ((0, 1), (2, 3)):
                    out = split_dot(
                        stacked([before_rows(prod[r, a] * grids[a]), before_rows(prod[r, b] * grids[b])]), tri[...]
                    )
                    for k, p in enumerate((a, b)):
                        grids[p] = bases[p] + out[k * TILE : (k + 1) * TILE]
            for p in range(PAIRS):
                final = prod[r, p] * grids[p]
                last[r, p] = final
                edge[r + 1, p] = bottoms[p] + all_rows(final)
            return carry

        lax.fori_loop(0, LEVELS, level, 0)

    def send_note(t):
        note[t] = rows_of_pairs([edge[LEVELS, p] for p in range(PAIRS)] + [corner[LEVELS, p] for p in range(PAIRS)])
        note_copy(t).start()

    def settle(t):
        tops = [edge[LEVELS, p] for p in range(PAIRS)]
        out = split_dot(stacked(tops), tri[...])
        whole = rows_of_pairs([corner[LEVELS, p] + tops[p] + out[8 * p : 8 * p + 8] for p in range(PAIRS)])
        top_ref[:, pl.ds(pl.multiple_of(t * TILE, TILE), TILE)] = whole[:PAIRS]

        def level(r, carry):
            out = split_dot(stacked([before_rows(last[r, p]) for p in range(PAIRS)]), ones[...])
            for p in range(PAIRS):
                lam[r, p] = lam[r, p] + out[p * TILE : (p + 1) * TILE]
            return carry

        lax.fori_loop(0, LEVELS, level, 0)
        ends = split_dot(stacked([edge[r, p] for r in range(LEVELS + 1) for p in range(PAIRS)] ), ones[...])
        for r in range(LEVELS + 1):
            for p in range(PAIRS):
                at = (r * PAIRS + p) * 8
                corner[r, p] = corner[r, p] + ends[at : at + 8]

    prepare(lambda n: y_ref[n])
    chain()

    def tick(t, carry):
        send_note(t)
        settle(t)
        y_copy(y_ref, t, 0, next1).wait_recv()

        @pl.when(t + 2 < HOPS)
        def _():
            y_copy(ybuf.at[t], t + 2, t + 2, next2).start()

        prepare(lambda n: ybuf[t, n])
        note_copy(t).wait_recv()
        got = heard[t]
        for p in range(PAIRS):
            rise = jnp.broadcast_to(got[p : p + 1], (8, TILE))
            from_corner = jnp.broadcast_to(got[PAIRS + p : PAIRS + p + 1], (8, TILE))
            rise = rise + jnp.where(lane_row == 0, from_corner - corner[0, p], 0.0)
            edge[0, p] = jnp.where(at_start, 0.0, rise)
        chain()
        return carry

    lax.fori_loop(0, HOPS, tick, 0)
    settle(HOPS)
    for r in range(LEVELS):
        found = []
        for p in range(PAIRS):
            row = all_rows(jnp.where(row_here == lane + 1, lam[r, p], 0.0)) + corner[r, p]
            found.append(jnp.where(lane_row == TILE - 1, corner[r + 1, p], row))
        right_ref[:, r * TILE : (r + 1) * TILE] = rows_of_pairs(found)[:PAIRS]

    x_copy().wait_send()
    for s in range(HOPS):
        y_copy(y_ref, s, s, next1).wait_send()
        note_copy(s).wait_send()


def local(x_path, x_anchor, y_steps, left_in, bottom_in, corner_in):
    tile = (LEVELS, PAIRS, TILE, TILE)
    row = (LEVELS + 1, PAIRS, 8, TILE)
    vmem = pl.BlockSpec(memory_space=pltpu.VMEM)
    dma = pltpu.SemaphoreType.DMA
    return pl.pallas_call(
        kernel,
        out_shape=(
            jax.ShapeDtypeStruct((PAIRS, LEVELS * TILE), F32),
            jax.ShapeDtypeStruct((PAIRS, TICKS * TILE), F32),
        ),
        in_specs=[vmem] * 6,
        out_specs=(vmem, vmem),
        scratch_shapes=[
            pltpu.VMEM(x_path.shape, BF16),
            *[pltpu.VMEM(tile, F32) for _ in range(6)],
            pltpu.VMEM(row, F32),
            pltpu.VMEM(row, F32),
            pltpu.VMEM((2 * TILE, TILE), BF16),
            pltpu.VMEM((2 * TILE, TILE), BF16),
            pltpu.VMEM((8, TILE), F32),
            pltpu.VMEM((8, TILE), F32),
            pltpu.VMEM((HOPS, *y_steps.shape), BF16),
            pltpu.VMEM((HOPS, 8, TILE), F32),
            pltpu.VMEM((HOPS, 8, TILE), F32),
            dma, dma, dma((HOPS,)), dma((HOPS,)), dma((HOPS,)), dma((HOPS,)),
        ],
        compiler_params=pltpu.CompilerParams(collective_id=0, has_side_effects=True, vmem_limit_bytes=40 * 1024 * 1024),
        name="goursat",
    )(x_path, x_anchor, y_steps, left_in, bottom_in, corner_in)


def solution(mesh):
    placed = (
        P("pair", "tm", None),
        P("pair", None),
        P("pair", "tm", None),
        P("pair", "tm"),
        P("pair", "tm"),
        P("pair", "tm"),
    )
    return jax.shard_map(
        local,
        mesh=mesh,
        in_specs=placed,
        out_specs=(P("pair", "tm"), P("pair", "tm")),
        check_vma=False,
    )
```

profile of v0, /device:TPU:16, one launch (start us, length us, event | category | flops | bytes accessed | tf_op | source)
XLA Modules:
  0.0 58.8 jit_solution(11781314743888409702)
XLA Ops:
  0.6 0.0 copy-start.3
  0.6 0.7 %copy.8.corner_ref = f32[4,1]{1,0:T(4,128)S(1)} copy(f32[4,1]{0,1:T(1,128)} %param.11) | data formatting | bytes 32 | tf_op args[5]
  1.4 0.0 copy-done.3
  1.4 0.0 copy-start
  1.4 1.2 %copy-done = bf16[2,512,512]{2,1,0:T(8,128)(2,1)S(1)} copy-done((bf16[2,512,512]{2,1,0:T(8,128)(2,1)S(1)}, bf16[2,512,512]{2,1,0:T(8,128)(2,1)}, u32[]{:S(2)}) %copy-start) | copy-done | bytes 1048600
  2.6 0.0 copy-start.1
  2.6 0.9 %copy-done.1 = bf16[2,128,512]{2,1,0:T(8,128)(2,1)S(1)} copy-done((bf16[2,128,512]{2,1,0:T(8,128)(2,1)S(1)}, bf16[2,128,512]{2,1,0:T(8,128)(2,1)}, u32[]{:S(2)}) %copy-start.1) | copy-done | bytes 262168
  3.6 0.0 copy-start.2
  3.6 0.7 %copy-done.2 = f32[4,512]{1,0:T(4,128)S(1)} copy-done((f32[4,512]{1,0:T(4,128)S(1)}, f32[4,512]{1,0:T(4,128)}, u32[]{:S(2)}) %copy-start.2) | copy-done | bytes 8216
  4.3 0.0 copy-start.4
  4.3 0.7 %copy-done.4 = f32[4,128]{1,0:T(4,128)S(1)} copy-done((f32[4,128]{1,0:T(4,128)S(1)}, f32[4,128]{1,0:T(4,128)}, u32[]{:S(2)}) %copy-start.4) | copy-done | bytes 2072
  4.9 52.6 %goursat.1 = (f32[4,512]{1,0:T(4,128)S(1)}, f32[4,768]{1,0:T(4,128)S(1)}) custom-call(bf16[2,512,512]{2,1,0:T(8,128)(2,1)S(1)} %copy-done, bf16[2,512]{1,0:T(2,128)(2,1)S(1)} %copy-done.3, bf16[2,128,512]{2,1,0:T(8,128)(2,1)S(1)} %copy-done.1, f32[4,512]{1,0:T(4,128)S(1)} %copy-done.2, f32[4,128]{1,0:T(4,128)S(1)} %copy-done.4, f32[4,1]{1,0:T(4,128)S(1)} %copy.8.corner_ref), custom_call_target="tpu_custom_call" | custom-call | tf_op jit(solution)/shard_map/goursat/pallas_call | solution.py:279
  57.6 0.6 %copy.11 = f32[4,512]{1,0:T(4,128)} copy(f32[4,512]{1,0:T(4,128)S(1)} %get-tuple-element.4) | data formatting | bytes 16384
  58.2 0.6 %copy.12 = f32[4,768]{1,0:T(4,128)} copy(f32[4,768]{1,0:T(4,128)S(1)} %get-tuple-element.5) | data formatting | bytes 24576
Async XLA Ops:
  0.6 0.8 %copy-start.3 = (bf16[2,512]{1,0:T(2,128)(2,1)S(1)}, bf16[2,512]{1,0:T(2,128)(2,1)}, u32[]{:S(2)}) copy-start(bf16[2,512]{1,0:T(2,128)(2,1)} %anchor_ref.1) | copy-start | bytes 6148
  1.4 1.2 %copy-start = (bf16[2,512,512]{2,1,0:T(8,128)(2,1)S(1)}, bf16[2,512,512]{2,1,0:T(8,128)(2,1)}, u32[]{:S(2)}) copy-start(bf16[2,512,512]{2,1,0:T(8,128)(2,1)} %x_ref.1) | copy-start | bytes 3145732
  2.6 0.9 %copy-start.1 = (bf16[2,128,512]{2,1,0:T(8,128)(2,1)S(1)}, bf16[2,128,512]{2,1,0:T(8,128)(2,1)}, u32[]{:S(2)}) copy-start(bf16[2,128,512]{2,1,0:T(8,128)(2,1)} %y_ref.1) | copy-start | bytes 786436
  3.6 0.7 %copy-start.2 = (f32[4,512]{1,0:T(4,128)S(1)}, f32[4,512]{1,0:T(4,128)}, u32[]{:S(2)}) copy-start(f32[4,512]{1,0:T(4,128)} %left_ref.1) | copy-start | bytes 24580
  4.3 0.7 %copy-start.4 = (f32[4,128]{1,0:T(4,128)S(1)}, f32[4,128]{1,0:T(4,128)}, u32[]{:S(2)}) copy-start(f32[4,128]{1,0:T(4,128)} %bottom_ref.1) | copy-start | bytes 6148
where the time goes:
time: 59 us; the launch traced here: 58.8 us
  Pallas kernels  52.6 us (89%)
  local copies, waits for them, and re-layouts  5.5 us (9%)
  between operations  0.65 us (1%)
    pallas_call x1, Pallas kernels, local(): pl.pallas_call(kernel, out_shape=(jax.ShapeDtypeStruct((PAIRS, LEVELS * T...  52.6 us
    unnamed x13, local copies, waits for them, and re-layouts  5.5 us

commit v1 on v0

--- a/solution.py
+++ b/solution.py
@@ -41,7 +41,7 @@
     return jnp.concatenate(parts, axis=0)
 
 
-def before_rows(tile):
+def before_rows(tile, start=None):
     sub = iota((8, TILE), 0)
     running = jnp.zeros((8, TILE), F32)
     sums = []
@@ -51,7 +51,7 @@
     scan = running
     for step in (1, 2, 4):
         scan = scan + jnp.where(sub >= step, pltpu.roll(scan, step, axis=0), 0.0)
-    offset = scan - running
+    offset = scan - running if start is None else scan - running + start
     return stacked([s + offset for s in sums])
 
 
@@ -78,8 +78,9 @@
 
 
 def kernel(
-    x_ref, anchor_ref, y_ref, left_ref, bottom_ref, corner_ref, right_ref, top_ref,
-    steps, prod, minus, plus, lead, lam, last, edge, corner, tri, ones,
+    x_hbm, anchor_hbm, y_hbm, left_hbm, bottom_hbm, corner_hbm, right_ref, top_ref,
+    x_ref, tail_ref, anchor_ref, y_ref, left_ref, bottom_ref, corner_ref, load,
+    steps, prod, minus, plus, lead, base, lam, last, edge, corner, tri, ones,
     xs, xgot, ybuf, note, heard,
     xs_send, xs_recv, y_send, y_recv, note_send, note_recv,
 ):
@@ -93,10 +94,20 @@
     for other in (prev1, prev2):
         pl.semaphore_signal(barrier, inc=1, device_id=(other, part), device_id_type=MESH)
 
-    for m in range(2):
-        tail = x_ref[m, 496:512, :].astype(F32)[15:16]
-        for c in range(4):
-            xs[m * 4 + c : m * 4 + c + 1, :] = tail[:, c * 128 : (c + 1) * 128]
+    loads = [
+        pltpu.make_async_copy(source, target, load.at[k])
+        for k, (source, target) in enumerate((
+            (x_hbm.at[:, LEVELS * TILE - 16 : LEVELS * TILE, :], tail_ref),
+            (y_hbm, y_ref),
+            (left_hbm, left_ref),
+            (bottom_hbm, bottom_ref),
+            (corner_hbm, corner_ref),
+            (x_hbm, x_ref),
+            (anchor_hbm, anchor_ref),
+        ))
+    ]
+    for copy in loads:
+        copy.start()
 
     def x_copy():
         return pltpu.make_async_remote_copy(
@@ -116,10 +127,20 @@
             device_id=(next1, part), device_id_type=MESH,
         )
 
+    loads[0].wait()
+    for m in range(2):
+        tail = tail_ref[m].astype(F32)[15:16]
+        for c in range(4):
+            xs[m * 4 + c : m * 4 + c + 1, :] = tail[:, c * 128 : (c + 1) * 128]
+    loads[1].wait()
+
     pl.semaphore_wait(barrier, 2)
-    x_copy().start()
+
+    @pl.when(me < count - 1)
+    def _():
+        x_copy().start()
+
     y_copy(y_ref, 0, 0, next1).start()
-    y_copy(y_ref, 1, 1, next2).start()
 
     from_row = iota((2 * TILE, TILE), 0) % TILE
     tri[...] = jnp.where(from_row < iota((2 * TILE, TILE), 1), 1.0, 0.0).astype(BF16)
@@ -128,8 +149,10 @@
     differ = jnp.where(lane == row_here, 1.0, jnp.where(lane == row_here - 1, -1.0, 0.0)).astype(BF16)
     lane_row = iota((8, TILE), 1)
 
+    for copy in loads[2:]:
+        copy.wait()
     for p in range(PAIRS):
-        start = jnp.broadcast_to(corner_ref[p : p + 1, 0:1], (8, TILE))
+        start = jnp.broadcast_to(corner_ref[0:1, p : p + 1], (8, TILE))
         start = jnp.where(at_start, 1.0, start)
         corner[0, p] = start
         for r in range(LEVELS):
@@ -152,67 +175,54 @@
         found = jnp.where(iota((TILE, 512), 0) == 0, found - previous, found)
         steps[m, r * TILE : (r + 1) * TILE, :] = found.astype(BF16)
 
-    for m in range(2):
-        for r in range(1, LEVELS):
-            increments(m, r, x_ref[m, r * TILE - 16 : r * TILE, :].astype(F32)[15:16])
-    x_copy().wait_recv()
-    for m in range(2):
-        came = jnp.concatenate([xgot[m * 4 + c : m * 4 + c + 1, :] for c in range(4)], axis=1)
-        increments(m, 0, jnp.where(at_start, anchor_ref[m : m + 1, :].astype(F32), came))
-
-    def prepare(y_of):
+    def products(y_of, first, last_level):
         for m in range(2):
             for n in range(2):
                 found = lax.dot_general(
-                    steps[m], y_of(n), (((1,), (1,)), ((), ())), preferred_element_type=F32
+                    steps[m, first * TILE : last_level * TILE, :], y_of(n), (((1,), (1,)), ((), ())),
+                    preferred_element_type=F32,
                 )
-                for r in range(LEVELS):
-                    prod[r, 2 * m + n] = found[r * TILE : (r + 1) * TILE]
-
-        def level(r, carry):
-            across = split_dot(stacked([prod[r, p] for p in range(PAIRS)]), tri[...])
-            for p in range(PAIRS):
-                wide = across[p * TILE : (p + 1) * TILE]
-                both = before_rows(wide)
-                down = before_rows(prod[r, p])
-                minus[r, p] = -(both + down)
-                plus[r, p] = 1.0 + both
-                edge_part = lam[r, p]
-                lead[r, p] = edge_part + before_rows(edge_part * wide)
-            return carry
-
-        lax.fori_loop(0, LEVELS, level, 0)
+                for r in range(first, last_level):
+                    prod[r, 2 * m + n] = found[(r - first) * TILE : (r - first + 1) * TILE]
+
+    def sums(r):
+        for p in range(PAIRS):
+            wide = split_dot(prod[r, p], tri[...])
+            both = before_rows(wide)
+            down = before_rows(prod[r, p])
+            minus[r, p] = -(both + down)
+            plus[r, p] = 1.0 + both
+            edge_part = lam[r, p]
+            lead[r, p] = edge_part + before_rows(edge_part * wide)
+            base[r, p] = edge_part + repeated(corner[r, p])
 
     def chain():
-        def level(r, carry):
+        def level(r):
             bottoms = [edge[r, p] for p in range(PAIRS)]
             rows = [repeated(bottoms[p]) * minus[r, p] for p in range(PAIRS)]
-            grids, bases = [None] * PAIRS, [None] * PAIRS
-            for a, b in ((0, 1), (2, 3)):
-                out = split_dot(stacked([rows[a], rows[b], bottoms[a], bottoms[b]]), tri[...])
-                for k, p in enumerate((a, b)):
-                    low = corner[r, p] + out[2 * TILE + 8 * k : 2 * TILE + 8 * k + 8]
-                    low = repeated(low)
-                    bases[p] = lam[r, p] + low
-                    grids[p] = lead[r, p] + low * plus[r, p] + out[k * TILE : (k + 1) * TILE]
+            grids = [None] * PAIRS
+            for p in range(PAIRS):
+                out = split_dot(stacked([rows[p], bottoms[p]]), tri[...])
+                low = repeated(corner[r, p] + out[TILE : TILE + 8])
+                grids[p] = lead[r, p] + low * plus[r, p] + out[:TILE]
             for sweep in range(2):
-                for a, b in ((0, 1), (2, 3)):
-                    out = split_dot(
-                        stacked([before_rows(prod[r, a] * grids[a]), before_rows(prod[r, b] * grids[b])]), tri[...]
-                    )
-                    for k, p in enumerate((a, b)):
-                        grids[p] = bases[p] + out[k * TILE : (k + 1) * TILE]
+                for p in range(PAIRS):
+                    inside = before_rows(prod[r, p] * grids[p], bottoms[p])
+                    grids[p] = base[r, p] + split_dot(inside, tri[...])
             for p in range(PAIRS):
                 final = prod[r, p] * grids[p]
                 last[r, p] = final
                 edge[r + 1, p] = bottoms[p] + all_rows(final)
-            return carry
-
-        lax.fori_loop(0, LEVELS, level, 0)
+
+        for r in range(LEVELS):
+            level(r)
 
     def send_note(t):
         note[t] = rows_of_pairs([edge[LEVELS, p] for p in range(PAIRS)] + [corner[LEVELS, p] for p in range(PAIRS)])
-        note_copy(t).start()
+
+        @pl.when(me < count - 1)
+        def _():
+            note_copy(t).start()
 
     def settle(t):
         tops = [edge[LEVELS, p] for p in range(PAIRS)]
@@ -220,20 +230,35 @@
         whole = rows_of_pairs([corner[LEVELS, p] + tops[p] + out[8 * p : 8 * p + 8] for p in range(PAIRS)])
         top_ref[:, pl.ds(pl.multiple_of(t * TILE, TILE), TILE)] = whole[:PAIRS]
 
-        def level(r, carry):
-            out = split_dot(stacked([before_rows(last[r, p]) for p in range(PAIRS)]), ones[...])
+        def level(r):
             for p in range(PAIRS):
-                lam[r, p] = lam[r, p] + out[p * TILE : (p + 1) * TILE]
-            return carry
-
-        lax.fori_loop(0, LEVELS, level, 0)
+                lam[r, p] = lam[r, p] + split_dot(before_rows(last[r, p]), ones[...])
+
+        for r in range(LEVELS):
+            level(r)
         ends = split_dot(stacked([edge[r, p] for r in range(LEVELS + 1) for p in range(PAIRS)] ), ones[...])
         for r in range(LEVELS + 1):
             for p in range(PAIRS):
                 at = (r * PAIRS + p) * 8
                 corner[r, p] = corner[r, p] + ends[at : at + 8]
 
-    prepare(lambda n: y_ref[n])
+    for m in range(2):
+        for r in range(1, LEVELS):
+            increments(m, r, x_ref[m, r * TILE - 16 : r * TILE, :].astype(F32)[15:16])
+    products(lambda n: y_ref[n], 1, LEVELS)
+    for r in range(1, LEVELS):
+        sums(r)
+    y_copy(y_ref, 1, 1, next2).start()
+
+    @pl.when(me > 0)
+    def _():
+        x_copy().wait_recv()
+
+    for m in range(2):
+        came = jnp.concatenate([xgot[m * 4 + c : m * 4 + c + 1, :] for c in range(4)], axis=1)
+        increments(m, 0, jnp.where(at_start, anchor_ref[m : m + 1, :].astype(F32), came))
+    products(lambda n: y_ref[n], 0, 1)
+    sums(0)
     chain()
 
     def tick(t, carry):
@@ -245,8 +270,14 @@
         def _():
             y_copy(ybuf.at[t], t + 2, t + 2, next2).start()
 
-        prepare(lambda n: ybuf[t, n])
-        note_copy(t).wait_recv()
+        products(lambda n: ybuf[t, n], 0, LEVELS)
+        for r in range(LEVELS):
+            sums(r)
+
+        @pl.when(me > 0)
+        def _():
+            note_copy(t).wait_recv()
+
         got = heard[t]
         for p in range(PAIRS):
             rise = jnp.broadcast_to(got[p : p + 1], (8, TILE))
@@ -265,16 +296,21 @@
             found.append(jnp.where(lane_row == TILE - 1, corner[r + 1, p], row))
         right_ref[:, r * TILE : (r + 1) * TILE] = rows_of_pairs(found)[:PAIRS]
 
-    x_copy().wait_send()
+    @pl.when(me < count - 1)
+    def _():
+        x_copy().wait_send()
+        for s in range(HOPS):
+            note_copy(s).wait_send()
+
     for s in range(HOPS):
         y_copy(y_ref, s, s, next1).wait_send()
-        note_copy(s).wait_send()
 
 
 def local(x_path, x_anchor, y_steps, left_in, bottom_in, corner_in):
     tile = (LEVELS, PAIRS, TILE, TILE)
     row = (LEVELS + 1, PAIRS, 8, TILE)
     vmem = pl.BlockSpec(memory_space=pltpu.VMEM)
+    hbm = pl.BlockSpec(memory_space=pltpu.HBM)
     dma = pltpu.SemaphoreType.DMA
     return pl.pallas_call(
         kernel,
@@ -282,11 +318,19 @@
             jax.ShapeDtypeStruct((PAIRS, LEVELS * TILE), F32),
             jax.ShapeDtypeStruct((PAIRS, TICKS * TILE), F32),
         ),
-        in_specs=[vmem] * 6,
+        in_specs=[hbm] * 6,
         out_specs=(vmem, vmem),
         scratch_shapes=[
             pltpu.VMEM(x_path.shape, BF16),
-            *[pltpu.VMEM(tile, F32) for _ in range(6)],
+            pltpu.VMEM((2, 16, x_path.shape[2]), BF16),
+            pltpu.VMEM(x_anchor.shape, BF16),
+            pltpu.VMEM(y_steps.shape, BF16),
+            pltpu.VMEM(left_in.shape, F32),
+            pltpu.VMEM(bottom_in.shape, F32),
+            pltpu.VMEM((1, PAIRS), F32),
+            dma((7,)),
+            pltpu.VMEM(x_path.shape, BF16),
+            *[pltpu.VMEM(tile, F32) for _ in range(7)],
             pltpu.VMEM(row, F32),
             pltpu.VMEM(row, F32),
             pltpu.VMEM((2 * TILE, TILE), BF16),
@@ -298,9 +342,9 @@
             pltpu.VMEM((HOPS, 8, TILE), F32),
             dma, dma, dma((HOPS,)), dma((HOPS,)), dma((HOPS,)), dma((HOPS,)),
         ],
-        compiler_params=pltpu.CompilerParams(collective_id=0, has_side_effects=True, vmem_limit_bytes=40 * 1024 * 1024),
+        compiler_params=pltpu.CompilerParams(collective_id=0, has_side_effects=True, vmem_limit_bytes=67043328),
         name="goursat",
-    )(x_path, x_anchor, y_steps, left_in, bottom_in, corner_in)
+    )(x_path, x_anchor, y_steps, left_in, bottom_in, corner_in.T)
 
 
 def solution(mesh):

time: 59 us -> 52.8 us (0.89)
  local copies, waits for them, and re-layouts: 5.5 us -> 1.9 us
  Pallas kernels: 52.6 us -> 50.1 us
    unnamed x13 -> x4, local copies, waits for them, and re-layouts: 5.5 us -> 1.9 us
    pallas_call x1, Pallas kernels: 52.6 us -> 50.1 us  [local(): pl.pallas_call(kernel, out_shape=(jax.ShapeDtypeStruct((PAIRS, LEVELS * T...]
where the time goes in v1:
time: 52.8 us; the launch traced here: 52.7 us
  Pallas kernels  50.1 us (95%)
  local copies, waits for them, and re-layouts  1.9 us (4%)
  between operations  0.65 us (1%)
    pallas_call x1, Pallas kernels, local(): pl.pallas_call(kernel, out_shape=(jax.ShapeDtypeStruct((PAIRS, LEVELS * T...  50.1 us
    unnamed x4, local copies, waits for them, and re-layouts  1.9 us

profile of v1, /device:TPU:16, one launch (start us, length us, event | category | flops | bytes accessed | tf_op | source)
XLA Modules:
  0.0 52.7 jit_solution(12696179719161935335)
XLA Ops:
  0.6 50.1 %goursat.1 = (f32[4,512]{1,0:T(4,128)}, f32[4,768]{1,0:T(4,128)}) custom-call(bf16[2,512,512]{2,1,0:T(8,128)(2,1)} %x_hbm.1, bf16[2,512]{1,0:T(2,128)(2,1)} %anchor_hbm.1, bf16[2,128,512]{2,1,0:T(8,128)(2,1)} %y_hbm.1, f32[4,512]{1,0:T(4,128)} %left_hbm.1, f32[4,128]{1,0:T(4,128)} %bottom_hbm.1, f32[1,4]{1,0:T(1,128)} %bitcast.1), custom_call_target="tpu_custom_call" | custom-call | tf_op jit(solution)/shard_map/goursat/pallas_call | solution.py:315
  50.8 0.0 copy-start
  50.8 1.3 %copy.10 = f32[4,512]{1,0:T(4,128)} copy(f32[4,512]{1,0:T(4,128)} %get-tuple-element.4) | data formatting | bytes 16384
  52.1 0.0 copy-done
  52.1 0.6 %copy.11 = f32[4,768]{1,0:T(4,128)} copy(f32[4,768]{1,0:T(4,128)S(1)} %copy-done) | data formatting | bytes 24576
Async XLA Ops:
  50.8 1.3 %copy-start = (f32[4,768]{1,0:T(4,128)S(1)}, f32[4,768]{1,0:T(4,128)}, u32[]{:S(2)}) copy-start(f32[4,768]{1,0:T(4,128)} %get-tuple-element.5) | copy-start | bytes 36868

commit v2 on v1

--- a/solution.py
+++ b/solution.py
@@ -248,7 +248,11 @@
     products(lambda n: y_ref[n], 1, LEVELS)
     for r in range(1, LEVELS):
         sums(r)
-    y_copy(y_ref, 1, 1, next2).start()
+
+    @pl.when(me < count - 2)
+    def _():
+        y_copy(y_ref, 1, 1, next2).start()
+
 
     @pl.when(me > 0)
     def _():
@@ -262,13 +266,32 @@
     chain()
 
     def tick(t, carry):
+        def arrival():
+            y_copy(y_ref, t, 0, next1).wait_recv()
+
+        def onward():
+            y_copy(ybuf.at[t], t + 2, t + 2, next2).start()
+
         send_note(t)
+
+        @pl.when(t > 0)
+        def _():
+            pl.when(t > 0)(arrival)
+
+            @pl.when(t + 2 < HOPS)
+            def _():
+                onward()
+
+        @pl.when((t == 0) & (me >= count - 2))
+        def _():
+            y_copy(y_ref, 1, 1, next2).start()
+
         settle(t)
-        y_copy(y_ref, t, 0, next1).wait_recv()
-
-        @pl.when(t + 2 < HOPS)
-        def _():
-            y_copy(ybuf.at[t], t + 2, t + 2, next2).start()
+
+        @pl.when(t == 0)
+        def _():
+            arrival()
+            onward()
 
         products(lambda n: ybuf[t, n], 0, LEVELS)
         for r in range(LEVELS):

time: 52.8 us -> 51 us (0.966)
  the two profiles are of different devices: /device:TPU:16 before, /device:TPU:8 now
where the time goes in v2:
time: 51 us; the launch traced here: 50.8 us
  Pallas kernels  48.3 us (95%)
  local copies, waits for them, and re-layouts  1.9 us (4%)
  between operations  0.65 us (1%)
    pallas_call x1, Pallas kernels, local(): pl.pallas_call(kernel, out_shape=(jax.ShapeDtypeStruct((PAIRS, LEVELS * T...  48.3 us
    unnamed x4, local copies, waits for them, and re-layouts  1.9 us

profile of v2, /device:TPU:8, one launch (start us, length us, event | category | flops | bytes accessed | tf_op | source)
XLA Modules:
  0.0 50.8 jit_solution(2432563281635774766)
XLA Ops:
  0.6 48.3 %goursat.1 = (f32[4,512]{1,0:T(4,128)}, f32[4,768]{1,0:T(4,128)}) custom-call(bf16[2,512,512]{2,1,0:T(8,128)(2,1)} %x_hbm.1, bf16[2,512]{1,0:T(2,128)(2,1)} %anchor_hbm.1, bf16[2,128,512]{2,1,0:T(8,128)(2,1)} %y_hbm.1, f32[4,512]{1,0:T(4,128)} %left_hbm.1, f32[4,128]{1,0:T(4,128)} %bottom_hbm.1, f32[1,4]{1,0:T(1,128)} %bitcast.1), custom_call_target="tpu_custom_call" | custom-call | tf_op jit(solution)/shard_map/goursat/pallas_call | solution.py:338
  48.9 0.0 copy-start
  48.9 1.3 %copy.10 = f32[4,512]{1,0:T(4,128)} copy(f32[4,512]{1,0:T(4,128)} %get-tuple-element.4) | data formatting | bytes 16384
  50.2 0.0 copy-done
  50.2 0.6 %copy.11 = f32[4,768]{1,0:T(4,128)} copy(f32[4,768]{1,0:T(4,128)S(1)} %copy-done) | data formatting | bytes 24576
Async XLA Ops:
  48.9 1.3 %copy-start = (f32[4,768]{1,0:T(4,128)S(1)}, f32[4,768]{1,0:T(4,128)}, u32[]{:S(2)}) copy-start(f32[4,768]{1,0:T(4,128)} %get-tuple-element.5) | copy-start | bytes 36868
